TPU v7x, 32 devices: a whole 2x2x4 slice. The times are simulated.
32 devices in a mesh: dp: 4 (over y, x), row: 2 (over core), col: 4 (over z).
Axes of the slice: x: 2, y: 2, z: 4, core: 2. Of those that a mesh axis runs over, the one named last changes fastest.
Arguments:
- tokens: bfloat16 [4096, 2048], P('dp', ('row', 'col')), may hold values from -40 to 40
- gain_attn: float32 [2048], P(('row', 'col')), may hold values from 0.5 to 1.5
- gain_ffn: float32 [2048], P(('row', 'col')), may hold values from 0.5 to 1.5
- w_query: bfloat16 [2048, 2048], P('row', 'col'), may hold values from -0.125 to 0.125
- w_key: bfloat16 [2048, 2048], P('row', 'col'), may hold values from -0.125 to 0.125
- w_value: bfloat16 [2048, 2048], P('row', 'col'), may hold values from -0.125 to 0.125
- w_out: bfloat16 [2048, 2048], P('col', 'row'), may hold values from -1 to 1
- w_gate: bfloat16 [2048, 8192], P('row', 'col'), may hold values from -0.125 to 0.125
- w_up: bfloat16 [2048, 8192], P('row', 'col'), may hold values from -0.125 to 0.125
- w_down: bfloat16 [8192, 2048], P('col', 'row'), may hold values from -0.0625 to 0.0625
- grad_output: bfloat16 [4096, 2048], P('dp', ('row', 'col')), may hold values from -6 to 6
- segments: int32 [4, 1024], P('dp'), may hold values from 0 to 2, as said below
- positions: int32 [4, 1024], P('dp'), may hold values from 0 to 2047, as said below
Outputs:
- output: float32 [4096, 2048], P('dp', ('row', 'col'))
- grad_tokens: float32 [4096, 2048], P('dp', ('row', 'col'))
- grad_gain_attn: float32 [8, 4, 64], P(('row', 'col'), 'dp')
- grad_gain_ffn: float32 [8, 4, 64], P(('row', 'col'), 'dp')
- grad_w_query: float32 [2, 4, 256, 2048], P('row', 'dp', None, 'col')
- grad_w_key: float32 [2, 4, 256, 2048], P('row', 'dp', None, 'col')
- grad_w_value: float32 [2, 4, 256, 2048], P('row', 'dp', None, 'col')
- grad_w_out: float32 [4, 4, 128, 2048], P('col', 'dp', None, 'row')
- grad_w_gate: float32 [2, 4, 256, 8192], P('row', 'dp', None, 'col')
- grad_w_up: float32 [2, 4, 256, 8192], P('row', 'dp', None, 'col')
- grad_w_down: float32 [4, 4, 512, 2048], P('col', 'dp', None, 'row')
Inputs may be any that keep to these rules, and one draw needn't show every extreme that they name: `segments`: within a sequence the numbers never fall; each sequence holds three documents. `positions`: positions count up by one inside a document; the first document of a sequence starts at a position no larger than 2048 minus its length, the others at 0.
All inputs are finite; a program needn't handle non-finite values.
Results may differ from a plain program's by a relative error of at most 0.015.
Values may be sent and summed in bfloat16 or wider, within the bound.
A program may use at most 256 MiB of HBM per device.

v0:
```python
import jax
import jax.numpy as jnp
from jax import lax
from jax.sharding import PartitionSpec as P

D = 2048
HD = 64
norm_eps = 1e-05
rope_base = 130000.0
masked_score = -1e30


def width_total(partial_sums):
    return lax.psum(partial_sums, ("row", "col"))


def gather_cols(pieces):
    return lax.all_gather(pieces, "col", axis=1, tiled=True)


def sum_cols(partial_sums):
    return lax.psum_scatter(partial_sums, "col", scatter_dimension=1, tiled=True)


def gather_rows(pieces):
    return lax.all_gather(pieces, "row", axis=2, tiled=True)


def sum_rows(partial_sums):
    return lax.psum_scatter(partial_sums, "row", scatter_dimension=2, tiled=True)


def product(left, right):
    return jnp.dot(left, right, preferred_element_type=jnp.float32)


def contract_rows(left, right):
    return jnp.einsum("ta,tb->ab", left, right, preferred_element_type=jnp.float32)


def times_transposed(left, right):
    return jnp.einsum("ta,ba->tb", left, right, preferred_element_type=jnp.float32)


def norm_forward(residual, gain_vec):
    squares = width_total(jnp.sum(residual * residual, axis=1))
    scale_inv = lax.rsqrt(squares / D + norm_eps)
    normed = residual * scale_inv[:, None]
    return (normed, scale_inv, (normed * gain_vec).astype(jnp.bfloat16))


def norm_backward(grad_normed_out, normed, scale_inv, gain_vec):
    grad_normed = grad_normed_out * gain_vec
    inner_sum = width_total(jnp.sum(grad_normed * normed, axis=1))
    grad_input = scale_inv[:, None] * (grad_normed - normed * (inner_sum / D)[:, None])
    return (grad_input, jnp.sum(grad_normed_out * normed, axis=0))


def rope_tables(positions):
    half_steps = jnp.arange(HD // 2, dtype=jnp.float32)
    inv_freq = rope_base ** (-2.0 * half_steps / HD)
    angles = positions.astype(jnp.float32)[:, None] * inv_freq[None, :]
    return (jnp.cos(angles)[:, None, :], jnp.sin(angles)[:, None, :])


def rotate(values, cos_table, sin_table):
    half_dim = values.shape[-1] // 2
    first_half = values[..., :half_dim]
    second_half = values[..., half_dim:]
    return jnp.concatenate(
        [
            first_half * cos_table - second_half * sin_table,
            second_half * cos_table + first_half * sin_table,
        ],
        axis=-1,
    )


def unrotate(values, cos_table, sin_table):
    half_dim = values.shape[-1] // 2
    first_half = values[..., :half_dim]
    second_half = values[..., half_dim:]
    return jnp.concatenate(
        [
            first_half * cos_table + second_half * sin_table,
            second_half * cos_table - first_half * sin_table,
        ],
        axis=-1,
    )


def score_rows(query_part, key_rows, segment, row_start):
    row_count = query_part.shape[0]
    seq_len = key_rows.shape[0]
    scores = jnp.einsum(
        "qhd,khd->hqk", query_part, key_rows, preferred_element_type=jnp.float32
    ) * key_rows.shape[2] ** (-0.5)
    query_slot = row_start + jnp.arange(row_count)
    key_slot = jnp.arange(seq_len)
    query_seg = segment[row_start : row_start + row_count]
    allowed = (key_slot[None, :] <= query_slot[:, None]) & (query_seg[:, None] == segment[None, :])
    return jnp.where(allowed[None], scores, masked_score)


def attend_forward(inputs):
    queries, key_rows, value_rows, segment = inputs
    seq_len = queries.shape[0]
    span = min(512, seq_len)
    results = []
    log_parts = []
    for row_start in range(0, seq_len, span):
        scores = score_rows(queries[row_start : row_start + span], key_rows, segment, row_start)
        log_total = jnp.log(jnp.sum(jnp.exp(scores), axis=-1))
        attn_probs = jnp.exp(scores - log_total[..., None]).astype(jnp.bfloat16)
        results.append(
            jnp.einsum("hqk,khd->qhd", attn_probs, value_rows, preferred_element_type=jnp.float32)
        )
        log_parts.append(log_total)
    return (jnp.concatenate(results, axis=0), jnp.concatenate(log_parts, axis=1))


def attend_backward(inputs):
    queries, key_rows, value_rows, segment, log_totals, grad_rows = inputs
    seq_len = queries.shape[0]
    span = min(512, seq_len)
    score_scale = queries.shape[2] ** (-0.5)
    grad_query_parts = []
    grad_keys = jnp.zeros(key_rows.shape, jnp.float32)
    grad_values = jnp.zeros(value_rows.shape, jnp.float32)
    for row_start in range(0, seq_len, span):
        query_part = queries[row_start : row_start + span]
        grad_part = grad_rows[row_start : row_start + span]
        scores = score_rows(query_part, key_rows, segment, row_start)
        attn_probs = jnp.exp(scores - log_totals[:, row_start : row_start + span, None])
        grad_probs = jnp.einsum(
            "qhd,khd->hqk", grad_part, value_rows, preferred_element_type=jnp.float32
        )
        weighted = jnp.sum(attn_probs * grad_probs, axis=-1, keepdims=True)
        grad_scores = (attn_probs * (grad_probs - weighted) * score_scale).astype(jnp.bfloat16)
        grad_query_parts.append(
            jnp.einsum("hqk,khd->qhd", grad_scores, key_rows, preferred_element_type=jnp.float32)
        )
        grad_keys = grad_keys + jnp.einsum(
            "hqk,qhd->khd", grad_scores, query_part, preferred_element_type=jnp.float32
        )
        grad_values = grad_values + jnp.einsum(
            "hqk,qhd->khd",
            attn_probs.astype(jnp.bfloat16),
            grad_part,
            preferred_element_type=jnp.float32,
        )
    return (jnp.concatenate(grad_query_parts, axis=0), grad_keys, grad_values)


def as_blocks(matrix):
    return matrix.reshape((1, 1) + matrix.shape)


def body(
    tokens,
    gain_attn,
    gain_ffn,
    w_query,
    w_key,
    w_value,
    w_out,
    w_gate,
    w_up,
    w_down,
    grad_output,
    segments,
    positions,
):
    residual = tokens.astype(jnp.float32)
    tok_count = residual.shape[0]
    seq_count, seq_len = segments.shape
    cos_table, sin_table = rope_tables(positions.reshape(tok_count))
    normed_one, inv_one, hidden_one = norm_forward(residual, gain_attn)
    gathered_one = gather_cols(hidden_one)
    projected = jnp.stack(
        [
            product(gathered_one, w_query),
            product(gathered_one, w_key),
            product(gathered_one, w_value),
        ]
    )
    local_qkv = sum_rows(projected)
    head_shape = (seq_count, seq_len, local_qkv.shape[2] // HD, HD)
    flat_heads = (tok_count, local_qkv.shape[2] // HD, HD)
    queries = (
        rotate(local_qkv[0].reshape(flat_heads), cos_table, sin_table)
        .astype(jnp.bfloat16)
        .reshape(head_shape)
    )
    key_rows = (
        rotate(local_qkv[1].reshape(flat_heads), cos_table, sin_table)
        .astype(jnp.bfloat16)
        .reshape(head_shape)
    )
    value_rows = local_qkv[2].astype(jnp.bfloat16).reshape(head_shape)
    attended, log_totals = lax.map(attend_forward, (queries, key_rows, value_rows, segments))
    heads_out = attended.reshape(tok_count, -1).astype(jnp.bfloat16)
    heads_all = gather_rows(heads_out[None])[0]
    middle = residual + sum_cols(product(heads_all, w_out))
    normed_two, inv_two, hidden_two = norm_forward(middle, gain_ffn)
    gathered_two = gather_cols(hidden_two)
    gate_up = sum_rows(jnp.stack([product(gathered_two, w_gate), product(gathered_two, w_up)]))
    gate_pre = gate_up[0]
    up_pre = gate_up[1]
    gate_sigmoid = jax.nn.sigmoid(gate_pre)
    hidden_units = (gate_pre * gate_sigmoid * up_pre).astype(jnp.bfloat16)
    units_all = gather_rows(hidden_units[None])[0]
    output = middle + sum_cols(product(units_all, w_down))
    grad_all = gather_cols(grad_output)
    units_all = gather_rows(hidden_units[None])[0]
    grad_w_down = contract_rows(units_all, grad_all)
    grad_units = sum_rows(times_transposed(grad_all, w_down)[None])[0]
    grad_gate = (
        grad_units * up_pre * gate_sigmoid * (1.0 + gate_pre * (1.0 - gate_sigmoid))
    ).astype(jnp.bfloat16)
    grad_up = (grad_units * gate_pre * gate_sigmoid).astype(jnp.bfloat16)
    gathered_two = gather_cols(hidden_two)
    grad_pair = gather_rows(jnp.stack([grad_gate, grad_up]))
    grad_w_gate = contract_rows(gathered_two, grad_pair[0])
    grad_w_up = contract_rows(gathered_two, grad_pair[1])
    grad_two = sum_cols(
        times_transposed(grad_pair[0], w_gate) + times_transposed(grad_pair[1], w_up)
    )
    grad_norm_two, grad_gain_ffn = norm_backward(grad_two, normed_two, inv_two, gain_ffn)
    grad_middle = grad_output.astype(jnp.float32) + grad_norm_two
    grad_branch = gather_cols(grad_middle.astype(jnp.bfloat16))
    heads_all = gather_rows(heads_out[None])[0]
    grad_w_out = contract_rows(heads_all, grad_branch)
    grad_heads = sum_rows(times_transposed(grad_branch, w_out)[None])[0].astype(jnp.bfloat16)
    grad_queries, grad_keys, grad_values = lax.map(
        attend_backward,
        (queries, key_rows, value_rows, segments, log_totals, grad_heads.reshape(head_shape)),
    )
    grad_query_pre = (
        unrotate(grad_queries.reshape(flat_heads), cos_table, sin_table)
        .reshape(tok_count, -1)
        .astype(jnp.bfloat16)
    )
    grad_key_pre = (
        unrotate(grad_keys.reshape(flat_heads), cos_table, sin_table)
        .reshape(tok_count, -1)
        .astype(jnp.bfloat16)
    )
    grad_value_pre = grad_values.reshape(tok_count, -1).astype(jnp.bfloat16)
    grad_triple = gather_rows(jnp.stack([grad_query_pre, grad_key_pre, grad_value_pre]))
    gathered_one = gather_cols(hidden_one)
    grad_w_query = contract_rows(gathered_one, grad_triple[0])
    grad_w_key = contract_rows(gathered_one, grad_triple[1])
    grad_w_value = contract_rows(gathered_one, grad_triple[2])
    grad_one = sum_cols(
        times_transposed(grad_triple[0], w_query)
        + times_transposed(grad_triple[1], w_key)
        + times_transposed(grad_triple[2], w_value)
    )
    grad_norm_one, grad_gain_attn = norm_backward(grad_one, normed_one, inv_one, gain_attn)
    grad_tokens = grad_middle + grad_norm_one
    reduced = (
        lax.psum_scatter(grad_gain_attn, "dp", scatter_dimension=0, tiled=True),
        lax.psum_scatter(grad_gain_ffn, "dp", scatter_dimension=0, tiled=True),
        lax.psum_scatter(grad_w_query, "dp", scatter_dimension=0, tiled=True),
        lax.psum_scatter(grad_w_key, "dp", scatter_dimension=0, tiled=True),
        lax.psum_scatter(grad_w_value, "dp", scatter_dimension=0, tiled=True),
        lax.psum_scatter(grad_w_out, "dp", scatter_dimension=0, tiled=True),
        lax.psum_scatter(grad_w_gate, "dp", scatter_dimension=0, tiled=True),
        lax.psum_scatter(grad_w_up, "dp", scatter_dimension=0, tiled=True),
        lax.psum_scatter(grad_w_down, "dp", scatter_dimension=0, tiled=True),
    )
    gate_share, up_share = (reduced[6], reduced[7])
    return (
        output,
        grad_tokens,
        as_blocks(reduced[0]),
        as_blocks(reduced[1]),
        as_blocks(reduced[2]),
        as_blocks(reduced[3]),
        as_blocks(reduced[4]),
        as_blocks(reduced[5]),
        as_blocks(gate_share),
        as_blocks(up_share),
        as_blocks(reduced[8]),
    )


def solution(mesh):
    return jax.shard_map(
        body,
        mesh=mesh,
        in_specs=(
            P("dp", ("row", "col")),
            P(("row", "col")),
            P(("row", "col")),
            P("row", "col"),
            P("row", "col"),
            P("row", "col"),
            P("col", "row"),
            P("row", "col"),
            P("row", "col"),
            P("col", "row"),
            P("dp", ("row", "col")),
            P("dp", None),
            P("dp", None),
        ),
        out_specs=(
            P("dp", ("row", "col")),
            P("dp", ("row", "col")),
            P(("row", "col"), "dp", None),
            P(("row", "col"), "dp", None),
            P("row", "dp", None, "col"),
            P("row", "dp", None, "col"),
            P("row", "dp", None, "col"),
            P("col", "dp", None, "row"),
            P("row", "dp", None, "col"),
            P("row", "dp", None, "col"),
            P("col", "dp", None, "row"),
        ),
        check_vma=False,
    )
```

profile of v0, /device:TPU:0, one launch (start us, length us, event | category | flops | bytes accessed | tf_op | source)
XLA Modules:
  0.0 1258.6 jit_solution(7421168657881235583)
XLA Ops:
  8.6 18.5 %psum.28 = f32[1024]{0:T(1024)S(1)} all-reduce(f32[1024]{0:T(1024)S(1)} %fusion.95), channel_id=1, replica_groups=mesh['dp'=4,'row'=2,'col'=4] {'row','col'}, use_global_device_ids=true, to_apply=%region_1.0 | all-reduce | flops 1024 | bytes 8192 | tf_op jit(solution)/shard_map/psum | solution.py:14
  29.3 44.6 %all-gather.9.cloned.1.call-done = bf16[1024,1024]{1,0:T(8,128)(2,1)} async-done(((bf16[1024,256]{1,0:T(8,128)(2,1)}), bf16[1024,1024]{1,0:T(8,128)(2,1)}) %all-gather.9.cloned.1.call-update) | async-done | bytes 2097168 | tf_op jit(solution)/shard_map/all_gather | solution.py:18
  86.2 9.1 reduce-scatter.16.cloned.1.call-done
  104.7 8.7 fusion.5
  113.5 7.0 fusion.4
  120.5 4.9 fusion.86
  128.6 10.4 all-gather.11.cloned.1.call-done
  144.1 77.5 %reduce-scatter.18.cloned.1.call-done = f32[1024,256]{1,0:T(8,128)} async-done(((f32[1024,1024]{1,0:T(8,128)}), f32[1024,256]{1,0:T(8,128)}) %reduce-scatter.18.cloned.1.call-update) | async-done | bytes 1048592 | tf_op jit(solution)/shard_map/reduce_scatter | solution.py:22
  223.1 16.6 %psum.29 = f32[1024]{0:T(1024)S(1)} all-reduce(f32[1024]{0:T(1024)S(1)} %get-tuple-element.68), channel_id=1, replica_groups=mesh['dp'=4,'row'=2,'col'=4] {'row','col'}, use_global_device_ids=true, to_apply=%region_7.8 | all-reduce | flops 1024 | bytes 8192 | tf_op jit(solution)/shard_map/psum | solution.py:14
  241.3 28.8 %all-gather.17.cloned.1.call-done = bf16[1024,1024]{1,0:T(8,128)(2,1)} async-done(((bf16[1024,256]{1,0:T(8,128)(2,1)}), bf16[1024,1024]{1,0:T(8,128)(2,1)}) %all-gather.17.cloned.1.call-update) | async-done | bytes 2097168 | tf_op jit(solution)/shard_map/all_gather | solution.py:18
  270.1 10.6 convolution_bitcast_fusion
  280.7 35.8 %all-gather.13.cloned.1.call-done = bf16[1024,1024]{1,0:T(8,128)(2,1)} async-done(((bf16[1024,256]{1,0:T(8,128)(2,1)}), bf16[1024,1024]{1,0:T(8,128)(2,1)}) %all-gather.13.cloned.1.call-update) | async-done | bytes 2097168 | tf_op jit(solution)/shard_map/all_gather | solution.py:18
  316.5 7.1 convolution_bitcast_fusion.1
  328.1 7.0 pad_maximum_fusion
  335.3 26.6 %reduce-scatter.20.cloned.1.call-done = f32[2,1024,1024]{2,1,0:T(8,128)} async-done(((f32[2,1024,2048]{2,1,0:T(8,128)}), f32[2,1024,1024]{2,1,0:T(8,128)}) %reduce-scatter.20.cloned.1.call-update) | async-done | bytes 8388624 | tf_op jit(solution)/shard_map/reduce_scatter | solution.py:30
  361.8 7.0 multiply_convert_fusion.3
  371.4 21.0 %all-gather.19.cloned.1.call-done = bf16[2,1024,2048]{2,1,0:T(8,128)(2,1)} async-done(((bf16[2,1024,1024]{2,1,0:T(8,128)(2,1)}), bf16[2,1024,2048]{2,1,0:T(8,128)(2,1)}) %all-gather.19.cloned.1.call-update) | async-done | bytes 8388624 | tf_op jit(solution)/shard_map/all_gather | solution.py:26
  392.4 7.9 fusion.41
  400.4 6.1 fusion.54
  406.6 78.1 %reduce-scatter.26.cloned.1.call-done = f32[1024,256]{1,0:T(8,128)} async-done(((f32[1024,1024]{1,0:T(8,128)}), f32[1024,256]{1,0:T(8,128)}) %reduce-scatter.26.cloned.1.call-update) | async-done | bytes 1048592 | tf_op jit(solution)/shard_map/reduce_scatter | solution.py:22
  486.3 16.0 %psum.30 = f32[1024]{0:T(1024)S(1)} all-reduce(f32[1024]{0:T(1024)S(1)} %get-tuple-element.53), channel_id=1, replica_groups=mesh['dp'=4,'row'=2,'col'=4] {'row','col'}, use_global_device_ids=true, to_apply=%region_13.14 | all-reduce | flops 1024 | bytes 8192 | tf_op jit(solution)/shard_map/psum | solution.py:14
  504.8 45.1 %all-gather.21.cloned.1.call-done = bf16[1024,1024]{1,0:T(8,128)(2,1)} async-done(((bf16[1024,256]{1,0:T(8,128)(2,1)}), bf16[1024,1024]{1,0:T(8,128)(2,1)}) %all-gather.21.cloned.1.call-update) | async-done | bytes 2097168 | tf_op jit(solution)/shard_map/all_gather | solution.py:18
  554.4 7.7 reduce-scatter.28.cloned.1.call-done
  563.6 4.5 fusion.132
  568.1 12.7 %fusion.29 = f32[4,64,1024]{2,1,0:T(8,128)} fusion(f32[4,512,1024]{2,1,0:T(8,128)} %fusion.5, f32[4,512,1024]{2,1,0:T(8,128)} %fusion.132, bf16[1024,4,32]{0,2,1:T(8,128)(2,1)S(1)} %copy-done.18, bf16[1024,4,32]{0,2,1:T(8,128)(2,1)S(1)} %copy-done.16), kind=kOutput, calls=%fused_computation.43 | convolution fusion | flops 279448576 | bytes 35127296 | tf_op jit(solution)/shard_map/while/body/eval_jaxpr/hqk,qhd->khd/dot_general | solution.py:143
  580.8 13.5 %fusion.74 = f32[512,4,64]{0,2,1:T(8,128)} fusion(f32[4,512,1024]{2,1,0:T(8,128)} %fusion.5, f32[4,512,1024]{2,1,0:T(8,128)} %fusion.132, bf16[1024,4,32]{0,2,1:T(8,128)(2,1)} %get-tuple-element.80, bf16[1024,4,32]{0,2,1:T(8,128)(2,1)S(1)} %copy-done.20), kind=kOutput, calls=%fused_computation.81 | convolution fusion | flops 279972864 | bytes 17825792 | tf_op jit(solution)/shard_map/while/body/eval_jaxpr/hqk,khd->qhd/dot_general | solution.py:141
  595.2 4.5 fusion.133
  604.0 12.0 fusion.71
  616.0 14.0 %fusion.65 = f32[1024,4,64]{0,2,1:T(8,128)} fusion(f32[4,64,1024]{2,1,0:T(8,128)} %fusion.29, f32[4,512,1024]{2,1,0:T(8,128)} %fusion.4, f32[4,512,1024]{2,1,0:T(8,128)} %fusion.133, bf16[1024,4,32]{0,2,1:T(8,128)(2,1)} %get-tuple-element.89, bf16[1024,4,32]{0,2,1:T(8,128)(2,1)} %get-tuple-element.90), kind=kOutput, calls=%fused_computation.78 | convolution fusion | flops 279710720 | bytes 19398656 | tf_op jit(solution)/shard_map/while/body/eval_jaxpr/hqk,qhd->khd/dot_general | solution.py:143
  637.2 12.5 all-gather.23.cloned.1.call-done
  658.9 7.7 all-gather.15.cloned.1.call-done
  666.6 10.1 fusion.20
  676.8 10.7 fusion.18
  692.9 10.6 fusion.40
  703.6 10.7 fusion.42
  714.4 4.5 fusion.104
  723.8 4.5 fusion.108
  729.7 17.1 %reduce-scatter.30.cloned.1.call-done = f32[1024,256]{1,0:T(8,128)} async-done(((f32[1024,1024]{1,0:T(8,128)}), f32[1024,256]{1,0:T(8,128)}) %reduce-scatter.30.cloned.1.call-update) | async-done | bytes 1048592 | tf_op jit(solution)/shard_map/reduce_scatter | solution.py:22
  748.5 9.8 all-reduce.2
  758.3 16.5 %psum.31 = f32[1024]{0:T(1024)S(1)} all-reduce(f32[1024]{0:T(1024)S(1)} %get-tuple-element.55), channel_id=1, replica_groups=mesh['dp'=4,'row'=2,'col'=4] {'row','col'}, use_global_device_ids=true, to_apply=%region_19.20 | all-reduce | flops 1024 | bytes 8192 | tf_op jit(solution)/shard_map/psum | solution.py:14
  776.0 50.8 %reduce-scatter.22.cloned.1.call-done = f32[1024,256]{1,0:T(8,128)} async-done(((f32[1024,1024]{1,0:T(8,128)}), f32[1024,256]{1,0:T(8,128)}) %reduce-scatter.22.cloned.1.call-update) | async-done | bytes 1048592 | tf_op jit(solution)/shard_map/reduce_scatter | solution.py:22
  830.0 87.1 %reduce-scatter.44.cloned.1.call-done = f32[512,1024]{1,0:T(8,128)} async-done(((f32[2048,1024]{1,0:T(8,128)}), f32[512,1024]{1,0:T(8,128)}) %reduce-scatter.44.cloned.1.call-update) | async-done | bytes 2097168 | tf_op jit(solution)/shard_map/reduce_scatter | solution.py:271
  917.1 38.6 %reduce-scatter.38.cloned.1.call-done = f32[128,1024]{1,0:T(8,128)} async-done(((f32[512,1024]{1,0:T(8,128)}), f32[128,1024]{1,0:T(8,128)}) %reduce-scatter.38.cloned.1.call-update) | async-done | bytes 524304 | tf_op jit(solution)/shard_map/reduce_scatter | solution.py:268
  955.7 90.0 %reduce-scatter.40.cloned.1.call-done = f32[256,2048]{1,0:T(8,128)} async-done(((f32[1024,2048]{1,0:T(8,128)}), f32[256,2048]{1,0:T(8,128)}) %reduce-scatter.40.cloned.1.call-update) | async-done | bytes 2097168 | tf_op jit(solution)/shard_map/reduce_scatter | solution.py:269
  1045.7 89.8 %reduce-scatter.42.cloned.1.call-done = f32[256,2048]{1,0:T(8,128)} async-done(((f32[1024,2048]{1,0:T(8,128)}), f32[256,2048]{1,0:T(8,128)}) %reduce-scatter.42.cloned.1.call-update) | async-done | bytes 2097168 | tf_op jit(solution)/shard_map/reduce_scatter | solution.py:270
  1135.6 38.8 %reduce-scatter.32.cloned.1.call-done = f32[256,512]{1,0:T(8,128)} async-done(((f32[1024,512]{1,0:T(8,128)}), f32[256,512]{1,0:T(8,128)}) %reduce-scatter.32.cloned.1.call-update) | async-done | bytes 524304 | tf_op jit(solution)/shard_map/reduce_scatter | solution.py:265
  1174.4 38.8 %reduce-scatter.34.cloned.1.call-done = f32[256,512]{1,0:T(8,128)} async-done(((f32[1024,512]{1,0:T(8,128)}), f32[256,512]{1,0:T(8,128)}) %reduce-scatter.34.cloned.1.call-update) | async-done | bytes 524304 | tf_op jit(solution)/shard_map/reduce_scatter | solution.py:266
  1213.1 38.8 %reduce-scatter.36.cloned.1.call-done = f32[256,512]{1,0:T(8,128)} async-done(((f32[1024,512]{1,0:T(8,128)}), f32[256,512]{1,0:T(8,128)}) %reduce-scatter.36.cloned.1.call-update) | async-done | bytes 524304 | tf_op jit(solution)/shard_map/reduce_scatter | solution.py:267
  (170 shorter events, 92.1 us)
Async XLA Ops:
  7.2 131.9 %copy-start = (bf16[512,1024]{1,0:T(8,128)(2,1)S(1)}, bf16[512,1024]{1,0:T(8,128)(2,1)}, u32[]{:S(2)}) copy-start(bf16[512,1024]{1,0:T(8,128)(2,1)} %param.19) | copy-start | bytes 3145732
  7.2 66.7 %all-gather.9.cloned.1.call-start = ((), (), s32[]{:S(2)}) async-start(), calls=%async_computation.15 | async-start | bytes 2621440 | tf_op jit(solution)/shard_map/all_gather | solution.py:18
  27.1 50.0 %copy-start.22 = (f32[1024]{0:T(1024)}, f32[1024]{0:T(1024)S(1)}, u32[]{:S(2)}) copy-start(f32[1024]{0:T(1024)S(1)} %add_rsqrt_fusion.1) | copy-start | bytes 12292
  29.2 47.9 %copy-start.34 = (bf16[1024,512]{1,0:T(8,128)(2,1)S(1)}, bf16[1024,512]{1,0:T(8,128)(2,1)}, u32[]{:S(2)}) copy-start(bf16[1024,512]{1,0:T(8,128)(2,1)} %param.17) | copy-start | bytes 3145732
  29.2 66.0 %reduce-scatter.16.cloned.1.call-start = ((), (), s32[]{:S(2)}) async-start(), calls=%async_computation.16 | async-start | bytes 9437184 | tf_op jit(solution)/shard_map/reduce_scatter | solution.py:30
  83.1 56.0 %all-gather.11.cloned.1.call-start = ((), (), s32[]{:S(2)}) async-start(), calls=%async_computation.17 | async-start | bytes 1572864 | tf_op jit(solution)/shard_map/all_gather | solution.py:26
  84.3 17.9 %copy-start.8 = (f32[1024,32]{0,1:T(8,128)}, f32[1024,32]{0,1:T(8,128)S(1)}, u32[]{:S(2)}) copy-start(f32[1024,32]{0,1:T(8,128)S(1)} %get-tuple-element.92) | copy-start | bytes 393220
  104.7 8.7 copy-start.12
  104.7 8.7 copy-start.15
  104.7 8.7 copy-start.17
  104.7 8.7 copy-start.19
  104.7 8.7 copy-start.21
  120.5 5.8 copy-start.2
  128.6 93.1 %reduce-scatter.18.cloned.1.call-start = ((), (), s32[]{:S(2)}) async-start(), calls=%async_computation.18 | async-start | bytes 5242880 | tf_op jit(solution)/shard_map/reduce_scatter | solution.py:22
  143.5 78.2 %copy-start.3 = (bf16[1024,256]{1,0:T(8,128)(2,1)S(1)}, bf16[1024,256]{1,0:T(8,128)(2,1)}, u32[]{:S(2)}) copy-start(bf16[1024,256]{1,0:T(8,128)(2,1)} %param.13) | copy-start | bytes 1572868
  143.5 96.2 %copy-start.24 = (f32[256]{0:T(256)S(1)}, f32[256]{0:T(256)}, u32[]{:S(2)}) copy-start(f32[256]{0:T(256)} %param.15) | copy-start | bytes 3076
  143.5 126.6 %all-gather.17.cloned.1.call-start = ((), (), s32[]{:S(2)}) async-start(), calls=%async_computation.23 | async-start | bytes 2621440 | tf_op jit(solution)/shard_map/all_gather | solution.py:18
  144.1 172.4 %all-gather.13.cloned.1.call-start = ((), (), s32[]{:S(2)}) async-start(), calls=%async_computation.19 | async-start | bytes 2621440 | tf_op jit(solution)/shard_map/all_gather | solution.py:18
  240.7 94.6 %reduce-scatter.24.cloned.1.call-start = ((), (), s32[]{:S(2)}) async-start(), calls=%async_computation.24 | async-start | bytes 12582912 | tf_op jit(solution)/shard_map/reduce_scatter | solution.py:30
  280.7 81.2 %reduce-scatter.20.cloned.1.call-start = ((), (), s32[]{:S(2)}) async-start(), calls=%async_computation.20 | async-start | bytes 25165824 | tf_op jit(solution)/shard_map/reduce_scatter | solution.py:30
  316.5 7.1 copy-start.29
  316.5 7.1 copy-start.32
  335.2 57.2 %all-gather.19.cloned.1.call-start = ((), (), s32[]{:S(2)}) async-start(), calls=%async_computation.25 | async-start | bytes 12582912 | tf_op jit(solution)/shard_map/all_gather | solution.py:26
  371.2 113.5 %reduce-scatter.26.cloned.1.call-start = ((), (), s32[]{:S(2)}) async-start(), calls=%async_computation.26 | async-start | bytes 5242880 | tf_op jit(solution)/shard_map/reduce_scatter | solution.py:22
  392.4 8.0 copy-start.28
  392.4 8.0 copy-start.30
  406.5 95.8 %copy-start.5 = (bf16[1024,256]{1,0:T(8,128)(2,1)S(1)}, bf16[1024,256]{1,0:T(8,128)(2,1)}, u32[]{:S(2)}) copy-start(bf16[1024,256]{1,0:T(8,128)(2,1)} %param.23) | copy-start | bytes 1572868
  406.6 143.4 %all-gather.21.cloned.1.call-start = ((), (), s32[]{:S(2)}) async-start(), calls=%async_computation.27 | async-start | bytes 2621440 | tf_op jit(solution)/shard_map/all_gather | solution.py:18
  504.7 57.4 %reduce-scatter.28.cloned.1.call-start = ((), (), s32[]{:S(2)}) async-start(), calls=%async_computation.28 | async-start | bytes 3145728 | tf_op jit(solution)/shard_map/reduce_scatter | solution.py:30
  554.2 95.6 %all-gather.23.cloned.1.call-start = ((), (), s32[]{:S(2)}) async-start(), calls=%async_computation.29 | async-start | bytes 4718592 | tf_op jit(solution)/shard_map/all_gather | solution.py:26
  563.6 4.5 copy-start.16
  563.6 4.5 copy-start.18
  568.1 12.7 %copy-start.20 = (bf16[1024,4,32]{0,2,1:T(8,128)(2,1)S(1)}, bf16[1024,4,32]{0,2,1:T(8,128)(2,1)}, u32[]{:S(2)}) copy-start(bf16[1024,4,32]{0,2,1:T(8,128)(2,1)} %get-tuple-element.79) | copy-start | bytes 786436
  636.2 30.4 %all-gather.15.cloned.1.call-start = ((), (), s32[]{:S(2)}) async-start(), calls=%async_computation.21 | async-start | bytes 6291456 | tf_op jit(solution)/shard_map/all_gather | solution.py:26
  636.8 109.9 %reduce-scatter.30.cloned.1.call-start = ((), (), s32[]{:S(2)}) async-start(), calls=%async_computation.30 | async-start | bytes 5242880 | tf_op jit(solution)/shard_map/reduce_scatter | solution.py:22
  658.8 168.0 %reduce-scatter.22.cloned.1.call-start = ((), (), s32[]{:S(2)}) async-start(), calls=%async_computation.22 | async-start | bytes 5242880 | tf_op jit(solution)/shard_map/reduce_scatter | solution.py:22
  676.7 240.4 %reduce-scatter.44.cloned.1.call-start = ((), (), s32[]{:S(2)}) async-start(), calls=%async_computation.37 | async-start | bytes 10485760 | tf_op jit(solution)/shard_map/reduce_scatter | solution.py:271
  687.5 268.3 %reduce-scatter.38.cloned.1.call-start = ((), (), s32[]{:S(2)}) async-start(), calls=%async_computation.34 | async-start | bytes 2621440 | tf_op jit(solution)/shard_map/reduce_scatter | solution.py:268
  692.8 352.9 %reduce-scatter.40.cloned.1.call-start = ((), (), s32[]{:S(2)}) async-start(), calls=%async_computation.35 | async-start | bytes 10485760 | tf_op jit(solution)/shard_map/reduce_scatter | solution.py:269
  703.6 432.0 %reduce-scatter.42.cloned.1.call-start = ((), (), s32[]{:S(2)}) async-start(), calls=%async_computation.36 | async-start | bytes 10485760 | tf_op jit(solution)/shard_map/reduce_scatter | solution.py:270
  714.4 460.0 %reduce-scatter.32.cloned.1.call-start = ((), (), s32[]{:S(2)}) async-start(), calls=%async_computation.31 | async-start | bytes 2621440 | tf_op jit(solution)/shard_map/reduce_scatter | solution.py:265
  719.0 494.2 %reduce-scatter.34.cloned.1.call-start = ((), (), s32[]{:S(2)}) async-start(), calls=%async_computation.32 | async-start | bytes 2621440 | tf_op jit(solution)/shard_map/reduce_scatter | solution.py:266
  723.7 4.6 copy-start.35
  723.7 23.0 %copy-start.4 = (bf16[1024,256]{1,0:T(8,128)(2,1)S(1)}, bf16[1024,256]{1,0:T(8,128)(2,1)}, u32[]{:S(2)}) copy-start(bf16[1024,256]{1,0:T(8,128)(2,1)} %param.13) | copy-start | bytes 1572868
  723.7 23.0 %copy-start.23 = (f32[1024]{0:T(1024)S(1)}, f32[1024]{0:T(1024)}, u32[]{:S(2)}) copy-start(f32[1024]{0:T(1024)} %copy-done.22) | copy-start | bytes 12292
  723.7 23.0 %copy-start.26 = (f32[256]{0:T(256)S(1)}, f32[256]{0:T(256)}, u32[]{:S(2)}) copy-start(f32[256]{0:T(256)} %param.14) | copy-start | bytes 3076
  723.8 528.1 %reduce-scatter.36.cloned.1.call-start = ((), (), s32[]{:S(2)}) async-start(), calls=%async_computation.33 | async-start | bytes 2621440 | tf_op jit(solution)/shard_map/reduce_scatter | solution.py:267
  728.9 522.9 %copy-start.1 = (bf16[512,1024]{1,0:T(8,128)(2,1)S(1)}, bf16[512,1024]{1,0:T(8,128)(2,1)}, u32[]{:S(2)}) copy-start(bf16[512,1024]{1,0:T(8,128)(2,1)} %param.19) | copy-start | bytes 3145732
  (11 other events, 26.6 us)
Sparse Core Ops, SparseCore 0:
  29.3 44.4 all-gather.8
  83.2 12.0 reduce-scatter.15
  128.7 10.2 all-gather.10
  143.6 77.9 reduce-scatter.17
  223.1 46.9 all-gather.16
  272.1 44.4 all-gather.12
  318.8 14.4 reduce-scatter.23
  335.6 26.1 reduce-scatter.19
  371.3 21.1 all-gather.18
  406.7 77.9 reduce-scatter.25
  504.9 45.0 all-gather.20
  554.3 7.7 reduce-scatter.27
  636.3 13.3 all-gather.22
  651.7 14.8 all-gather.14
  668.7 77.9 reduce-scatter.29
  748.9 77.9 reduce-scatter.21
  830.3 86.7 reduce-scatter.43
  920.5 35.1 reduce-scatter.37
  959.4 86.3 reduce-scatter.39
  1049.2 86.3 reduce-scatter.41
  1139.1 35.1 reduce-scatter.31
  1177.9 35.1 reduce-scatter.33
  1216.7 35.1 reduce-scatter.35
where the time goes:
time: 1260 us
  waiting for transfers between devices  896 us (71%)
  matrix products  211 us (17%)
  blocking collectives  77.5 us (6%)
  other arithmetic  43.2 us (3%)
  between operations  15.5 us (1%)
    reduce_scatter x4, waiting for transfers between devices, sum_cols(): lax.psum_scatter(partial_sums, 'col', scatter_dimension=1, tiled=True)  223 us
    all_gather x4, waiting for transfers between devices, gather_cols(): return lax.all_gather(pieces, 'col', axis=1, tiled=True)  154 us
    reduce_scatter x1, waiting for transfers between devices, body(): lax.psum_scatter(grad_w_gate, 'dp', scatter_dimension=0, tiled=True)  90 us
    reduce_scatter x1, waiting for transfers between devices, body(): lax.psum_scatter(grad_w_up, 'dp', scatter_dimension=0, tiled=True)  89.8 us
    reduce_scatter x1, waiting for transfers between devices, body(): lax.psum_scatter(grad_w_down, 'dp', scatter_dimension=0, tiled=True)  87.1 us
    psum x4, blocking collectives, width_total(): return lax.psum(partial_sums, ('row', 'col'))  67.6 us
    all_gather x4, waiting for transfers between devices, gather_rows(): return lax.all_gather(pieces, 'row', axis=2, tiled=True)  51.7 us
    dot_general x7, matrix products, contract_rows(): jnp.einsum('ta,tb->ab', left, right, preferred_element_type=jnp.float32)  49.7 us
  transfers between devices with their start and end apart: 23, of which 22 were waited for; matrix products, arithmetic and copies ran while one was open for 9% of the time, Pallas kernels for 0%

commit v1 on v0

--- a/solution.py
+++ b/solution.py
@@ -11,7 +11,7 @@
 
 
 def width_total(partial_sums):
-    return lax.psum(partial_sums, ("row", "col"))
+    return jnp.sum(lax.all_gather(partial_sums, ("row", "col")), axis=0)
 
 
 def gather_cols(pieces):

time: 1260 us -> 1280 us (1.016)
  blocking collectives: 77.5 us -> 114 us
  waiting for transfers between devices: 896 us -> 879 us
    all_gather x0 -> x4, blocking collectives: none -> 104 us  [width_total(): return jnp.sum(lax.all_gather(partial_sums, ('row', 'col')), axis=0)]
    psum x4 -> x0, blocking collectives: 67.6 us -> none  [width_total(): return lax.psum(partial_sums, ('row', 'col'))]
where the time goes in v1:
time: 1280 us
  waiting for transfers between devices  879 us (69%)
  matrix products  211 us (16%)
  blocking collectives  114 us (9%)
  other arithmetic  43.3 us (3%)
  between operations  15.6 us (1%)
    reduce_scatter x4, waiting for transfers between devices, sum_cols(): lax.psum_scatter(partial_sums, 'col', scatter_dimension=1, tiled=True)  212 us
    all_gather x4, waiting for transfers between devices, gather_cols(): return lax.all_gather(pieces, 'col', axis=1, tiled=True)  149 us
    all_gather x4, blocking collectives, width_total(): return jnp.sum(lax.all_gather(partial_sums, ('row', 'col')), axis=0)  104 us
    reduce_scatter x1, waiting for transfers between devices, body(): lax.psum_scatter(grad_w_gate, 'dp', scatter_dimension=0, tiled=True)  90 us
    reduce_scatter x1, waiting for transfers between devices, body(): lax.psum_scatter(grad_w_up, 'dp', scatter_dimension=0, tiled=True)  89.8 us
    reduce_scatter x1, waiting for transfers between devices, body(): lax.psum_scatter(grad_w_down, 'dp', scatter_dimension=0, tiled=True)  87.1 us
    all_gather x4, waiting for transfers between devices, gather_rows(): return lax.all_gather(pieces, 'row', axis=2, tiled=True)  51.7 us
    dot_general x7, matrix products, contract_rows(): jnp.einsum('ta,tb->ab', left, right, preferred_element_type=jnp.float32)  49.7 us
  transfers between devices with their start and end apart: 23, of which 22 were waited for; matrix products, arithmetic and copies ran while one was open for 9% of the time, Pallas kernels for 0%

profile of v1, /device:TPU:0, one launch (start us, length us, event | category | flops | bytes accessed | tf_op | source)
XLA Modules:
  0.0 1278.4 jit_solution(17313869176664772305)
XLA Ops:
  8.6 25.2 %all-gather = f32[8192]{0:T(1024)S(1)} all-gather(f32[1024]{0:T(1024)S(1)} %fusion.95), channel_id=2, replica_groups=mesh['dp'=4,'row'=2,'col'=4] {'row','col'}, dimensions={0}, use_global_device_ids=true | all-gather | bytes 36864 | tf_op jit(solution)/shard_map/all_gather | solution.py:14
  36.0 47.7 %all-gather.13.cloned.1.call-done = bf16[1024,1024]{1,0:T(8,128)(2,1)} async-done(((bf16[1024,256]{1,0:T(8,128)(2,1)}), bf16[1024,1024]{1,0:T(8,128)(2,1)}) %all-gather.13.cloned.1.call-update) | async-done | bytes 2097168 | tf_op jit(solution)/shard_map/all_gather | solution.py:18
  96.0 9.0 reduce-scatter.16.cloned.1.call-done
  114.6 8.7 fusion.5
  123.3 7.0 fusion.4
  130.4 4.9 fusion.86
  138.5 10.4 all-gather.15.cloned.1.call-done
  154.0 77.5 %reduce-scatter.18.cloned.1.call-done = f32[1024,256]{1,0:T(8,128)} async-done(((f32[1024,1024]{1,0:T(8,128)}), f32[1024,256]{1,0:T(8,128)}) %reduce-scatter.18.cloned.1.call-update) | async-done | bytes 1048592 | tf_op jit(solution)/shard_map/reduce_scatter | solution.py:22
  232.9 27.1 %all-gather.1 = f32[8192]{0:T(1024)S(1)} all-gather(f32[1024]{0:T(1024)S(1)} %get-tuple-element.68), channel_id=3, replica_groups=mesh['dp'=4,'row'=2,'col'=4] {'row','col'}, dimensions={0}, use_global_device_ids=true | all-gather | bytes 36864 | tf_op jit(solution)/shard_map/all_gather | solution.py:14
  261.7 18.4 %all-gather.21.cloned.1.call-done = bf16[1024,1024]{1,0:T(8,128)(2,1)} async-done(((bf16[1024,256]{1,0:T(8,128)(2,1)}), bf16[1024,1024]{1,0:T(8,128)(2,1)}) %all-gather.21.cloned.1.call-update) | async-done | bytes 2097168 | tf_op jit(solution)/shard_map/all_gather | solution.py:18
  280.1 10.6 convolution_bitcast_fusion
  290.7 36.3 %all-gather.17.cloned.1.call-done = bf16[1024,1024]{1,0:T(8,128)(2,1)} async-done(((bf16[1024,256]{1,0:T(8,128)(2,1)}), bf16[1024,1024]{1,0:T(8,128)(2,1)}) %all-gather.17.cloned.1.call-update) | async-done | bytes 2097168 | tf_op jit(solution)/shard_map/all_gather | solution.py:18
  327.0 7.1 convolution_bitcast_fusion.1
  338.6 7.0 pad_maximum_fusion
  345.7 26.6 %reduce-scatter.20.cloned.1.call-done = f32[2,1024,1024]{2,1,0:T(8,128)} async-done(((f32[2,1024,2048]{2,1,0:T(8,128)}), f32[2,1024,1024]{2,1,0:T(8,128)}) %reduce-scatter.20.cloned.1.call-update) | async-done | bytes 8388624 | tf_op jit(solution)/shard_map/reduce_scatter | solution.py:30
  372.3 7.0 multiply_convert_fusion.3
  381.8 21.0 %all-gather.23.cloned.1.call-done = bf16[2,1024,2048]{2,1,0:T(8,128)(2,1)} async-done(((bf16[2,1024,1024]{2,1,0:T(8,128)(2,1)}), bf16[2,1024,2048]{2,1,0:T(8,128)(2,1)}) %all-gather.23.cloned.1.call-update) | async-done | bytes 8388624 | tf_op jit(solution)/shard_map/all_gather | solution.py:26
  402.9 7.9 fusion.41
  410.8 6.1 fusion.54
  417.1 78.1 %reduce-scatter.26.cloned.1.call-done = f32[1024,256]{1,0:T(8,128)} async-done(((f32[1024,1024]{1,0:T(8,128)}), f32[1024,256]{1,0:T(8,128)}) %reduce-scatter.26.cloned.1.call-update) | async-done | bytes 1048592 | tf_op jit(solution)/shard_map/reduce_scatter | solution.py:22
  496.8 24.1 %all-gather.2 = f32[8192]{0:T(1024)S(1)} all-gather(f32[1024]{0:T(1024)S(1)} %get-tuple-element.53), channel_id=4, replica_groups=mesh['dp'=4,'row'=2,'col'=4] {'row','col'}, dimensions={0}, use_global_device_ids=true | all-gather | bytes 36864 | tf_op jit(solution)/shard_map/all_gather | solution.py:14
  523.4 46.5 %all-gather.25.cloned.1.call-done = bf16[1024,1024]{1,0:T(8,128)(2,1)} async-done(((bf16[1024,256]{1,0:T(8,128)(2,1)}), bf16[1024,1024]{1,0:T(8,128)(2,1)}) %all-gather.25.cloned.1.call-update) | async-done | bytes 2097168 | tf_op jit(solution)/shard_map/all_gather | solution.py:18
  574.4 7.7 reduce-scatter.28.cloned.1.call-done
  583.5 4.5 fusion.132
  588.1 12.7 fusion.29
  600.7 13.5 %fusion.74 = f32[512,4,64]{0,2,1:T(8,128)} fusion(f32[4,512,1024]{2,1,0:T(8,128)} %fusion.5, f32[4,512,1024]{2,1,0:T(8,128)} %fusion.132, bf16[1024,4,32]{0,2,1:T(8,128)(2,1)} %get-tuple-element.80, bf16[1024,4,32]{0,2,1:T(8,128)(2,1)S(1)} %copy-done.20), kind=kOutput, calls=%fused_computation.81 | convolution fusion | flops 279972864 | bytes 17825792 | tf_op jit(solution)/shard_map/while/body/eval_jaxpr/hqk,khd->qhd/dot_general | solution.py:141
  615.1 4.5 fusion.133
  623.9 12.0 fusion.71
  636.0 14.0 %fusion.65 = f32[1024,4,64]{0,2,1:T(8,128)} fusion(f32[4,64,1024]{2,1,0:T(8,128)} %fusion.29, f32[4,512,1024]{2,1,0:T(8,128)} %fusion.4, f32[4,512,1024]{2,1,0:T(8,128)} %fusion.133, bf16[1024,4,32]{0,2,1:T(8,128)(2,1)} %get-tuple-element.89, bf16[1024,4,32]{0,2,1:T(8,128)(2,1)} %get-tuple-element.90), kind=kOutput, calls=%fused_computation.78 | convolution fusion | flops 279710720 | bytes 19398656 | tf_op jit(solution)/shard_map/while/body/eval_jaxpr/hqk,qhd->khd/dot_general | solution.py:143
  657.2 12.5 all-gather.27.cloned.1.call-done
  678.8 7.7 all-gather.19.cloned.1.call-done
  686.6 10.1 fusion.20
  696.8 10.7 fusion.18
  712.9 10.6 fusion.40
  723.6 10.7 fusion.42
  734.4 4.5 fusion.104
  743.8 4.5 fusion.108
  749.7 17.1 %reduce-scatter.30.cloned.1.call-done = f32[1024,256]{1,0:T(8,128)} async-done(((f32[1024,1024]{1,0:T(8,128)}), f32[1024,256]{1,0:T(8,128)}) %reduce-scatter.30.cloned.1.call-update) | async-done | bytes 1048592 | tf_op jit(solution)/shard_map/reduce_scatter | solution.py:22
  768.5 27.7 %all-gather.3 = f32[8192]{0:T(1024)S(1)} all-gather(f32[1024]{0:T(1024)S(1)} %get-tuple-element.55), channel_id=5, replica_groups=mesh['dp'=4,'row'=2,'col'=4] {'row','col'}, dimensions={0}, use_global_device_ids=true | all-gather | bytes 36864 | tf_op jit(solution)/shard_map/all_gather | solution.py:14
  796.2 9.8 all-reduce.2
  807.2 39.5 %reduce-scatter.22.cloned.1.call-done = f32[1024,256]{1,0:T(8,128)} async-done(((f32[1024,1024]{1,0:T(8,128)}), f32[1024,256]{1,0:T(8,128)}) %reduce-scatter.22.cloned.1.call-update) | async-done | bytes 1048592 | tf_op jit(solution)/shard_map/reduce_scatter | solution.py:22
  849.8 87.1 %reduce-scatter.44.cloned.1.call-done = f32[512,1024]{1,0:T(8,128)} async-done(((f32[2048,1024]{1,0:T(8,128)}), f32[512,1024]{1,0:T(8,128)}) %reduce-scatter.44.cloned.1.call-update) | async-done | bytes 2097168 | tf_op jit(solution)/shard_map/reduce_scatter | solution.py:271
  936.9 38.6 %reduce-scatter.38.cloned.1.call-done = f32[128,1024]{1,0:T(8,128)} async-done(((f32[512,1024]{1,0:T(8,128)}), f32[128,1024]{1,0:T(8,128)}) %reduce-scatter.38.cloned.1.call-update) | async-done | bytes 524304 | tf_op jit(solution)/shard_map/reduce_scatter | solution.py:268
  975.5 90.0 %reduce-scatter.40.cloned.1.call-done = f32[256,2048]{1,0:T(8,128)} async-done(((f32[1024,2048]{1,0:T(8,128)}), f32[256,2048]{1,0:T(8,128)}) %reduce-scatter.40.cloned.1.call-update) | async-done | bytes 2097168 | tf_op jit(solution)/shard_map/reduce_scatter | solution.py:269
  1065.5 89.8 %reduce-scatter.42.cloned.1.call-done = f32[256,2048]{1,0:T(8,128)} async-done(((f32[1024,2048]{1,0:T(8,128)}), f32[256,2048]{1,0:T(8,128)}) %reduce-scatter.42.cloned.1.call-update) | async-done | bytes 2097168 | tf_op jit(solution)/shard_map/reduce_scatter | solution.py:270
  1155.3 38.8 %reduce-scatter.32.cloned.1.call-done = f32[256,512]{1,0:T(8,128)} async-done(((f32[1024,512]{1,0:T(8,128)}), f32[256,512]{1,0:T(8,128)}) %reduce-scatter.32.cloned.1.call-update) | async-done | bytes 524304 | tf_op jit(solution)/shard_map/reduce_scatter | solution.py:265
  1194.1 38.8 %reduce-scatter.34.cloned.1.call-done = f32[256,512]{1,0:T(8,128)} async-done(((f32[1024,512]{1,0:T(8,128)}), f32[256,512]{1,0:T(8,128)}) %reduce-scatter.34.cloned.1.call-update) | async-done | bytes 524304 | tf_op jit(solution)/shard_map/reduce_scatter | solution.py:266
  1232.9 38.8 %reduce-scatter.36.cloned.1.call-done = f32[256,512]{1,0:T(8,128)} async-done(((f32[1024,512]{1,0:T(8,128)}), f32[256,512]{1,0:T(8,128)}) %reduce-scatter.36.cloned.1.call-update) | async-done | bytes 524304 | tf_op jit(solution)/shard_map/reduce_scatter | solution.py:267
  (178 shorter events, 92.2 us)
Async XLA Ops:
  7.2 141.7 %copy-start = (bf16[512,1024]{1,0:T(8,128)(2,1)S(1)}, bf16[512,1024]{1,0:T(8,128)(2,1)}, u32[]{:S(2)}) copy-start(bf16[512,1024]{1,0:T(8,128)(2,1)} %param.19) | copy-start | bytes 3145732
  7.2 76.5 %all-gather.13.cloned.1.call-start = ((), (), s32[]{:S(2)}) async-start(), calls=%async_computation.15 | async-start | bytes 2621440 | tf_op jit(solution)/shard_map/all_gather | solution.py:18
  33.9 53.1 %copy-start.22 = (f32[1024]{0:T(1024)}, f32[1024]{0:T(1024)S(1)}, u32[]{:S(2)}) copy-start(f32[1024]{0:T(1024)S(1)} %add_rsqrt_fusion.1) | copy-start | bytes 12292
  35.9 51.1 %copy-start.34 = (bf16[1024,512]{1,0:T(8,128)(2,1)S(1)}, bf16[1024,512]{1,0:T(8,128)(2,1)}, u32[]{:S(2)}) copy-start(bf16[1024,512]{1,0:T(8,128)(2,1)} %param.17) | copy-start | bytes 3145732
  36.0 69.1 %reduce-scatter.16.cloned.1.call-start = ((), (), s32[]{:S(2)}) async-start(), calls=%async_computation.16 | async-start | bytes 9437184 | tf_op jit(solution)/shard_map/reduce_scatter | solution.py:30
  92.9 56.0 %all-gather.15.cloned.1.call-start = ((), (), s32[]{:S(2)}) async-start(), calls=%async_computation.17 | async-start | bytes 1572864 | tf_op jit(solution)/shard_map/all_gather | solution.py:26
  94.2 17.9 %copy-start.8 = (f32[1024,32]{0,1:T(8,128)}, f32[1024,32]{0,1:T(8,128)S(1)}, u32[]{:S(2)}) copy-start(f32[1024,32]{0,1:T(8,128)S(1)} %get-tuple-element.92) | copy-start | bytes 393220
  114.6 8.7 copy-start.12
  114.6 8.7 copy-start.15
  114.6 8.7 copy-start.17
  114.6 8.7 copy-start.19
  114.6 8.7 copy-start.21
  130.4 5.8 copy-start.2
  138.4 93.1 %reduce-scatter.18.cloned.1.call-start = ((), (), s32[]{:S(2)}) async-start(), calls=%async_computation.18 | async-start | bytes 5242880 | tf_op jit(solution)/shard_map/reduce_scatter | solution.py:22
  153.3 78.2 %copy-start.3 = (bf16[1024,256]{1,0:T(8,128)(2,1)S(1)}, bf16[1024,256]{1,0:T(8,128)(2,1)}, u32[]{:S(2)}) copy-start(bf16[1024,256]{1,0:T(8,128)(2,1)} %param.13) | copy-start | bytes 1572868
  153.3 106.7 %copy-start.24 = (f32[256]{0:T(256)S(1)}, f32[256]{0:T(256)}, u32[]{:S(2)}) copy-start(f32[256]{0:T(256)} %param.15) | copy-start | bytes 3076
  153.4 126.7 %all-gather.21.cloned.1.call-start = ((), (), s32[]{:S(2)}) async-start(), calls=%async_computation.23 | async-start | bytes 2621440 | tf_op jit(solution)/shard_map/all_gather | solution.py:18
  154.0 173.0 %all-gather.17.cloned.1.call-start = ((), (), s32[]{:S(2)}) async-start(), calls=%async_computation.19 | async-start | bytes 2621440 | tf_op jit(solution)/shard_map/all_gather | solution.py:18
  261.1 84.6 %reduce-scatter.24.cloned.1.call-start = ((), (), s32[]{:S(2)}) async-start(), calls=%async_computation.24 | async-start | bytes 12582912 | tf_op jit(solution)/shard_map/reduce_scatter | solution.py:30
  290.7 81.6 %reduce-scatter.20.cloned.1.call-start = ((), (), s32[]{:S(2)}) async-start(), calls=%async_computation.20 | async-start | bytes 25165824 | tf_op jit(solution)/shard_map/reduce_scatter | solution.py:30
  327.0 7.1 copy-start.29
  327.0 7.1 copy-start.32
  345.6 57.3 %all-gather.23.cloned.1.call-start = ((), (), s32[]{:S(2)}) async-start(), calls=%async_computation.25 | async-start | bytes 12582912 | tf_op jit(solution)/shard_map/all_gather | solution.py:26
  381.6 113.5 %reduce-scatter.26.cloned.1.call-start = ((), (), s32[]{:S(2)}) async-start(), calls=%async_computation.26 | async-start | bytes 5242880 | tf_op jit(solution)/shard_map/reduce_scatter | solution.py:22
  402.9 8.0 copy-start.28
  402.9 8.0 copy-start.30
  417.0 103.9 %copy-start.5 = (bf16[1024,256]{1,0:T(8,128)(2,1)S(1)}, bf16[1024,256]{1,0:T(8,128)(2,1)}, u32[]{:S(2)}) copy-start(bf16[1024,256]{1,0:T(8,128)(2,1)} %param.23) | copy-start | bytes 1572868
  417.0 152.9 %all-gather.25.cloned.1.call-start = ((), (), s32[]{:S(2)}) async-start(), calls=%async_computation.27 | async-start | bytes 2621440 | tf_op jit(solution)/shard_map/all_gather | solution.py:18
  523.3 58.7 %reduce-scatter.28.cloned.1.call-start = ((), (), s32[]{:S(2)}) async-start(), calls=%async_computation.28 | async-start | bytes 3145728 | tf_op jit(solution)/shard_map/reduce_scatter | solution.py:30
  574.1 95.6 %all-gather.27.cloned.1.call-start = ((), (), s32[]{:S(2)}) async-start(), calls=%async_computation.29 | async-start | bytes 4718592 | tf_op jit(solution)/shard_map/all_gather | solution.py:26
  583.5 4.5 copy-start.16
  583.5 4.5 copy-start.18
  588.1 12.7 copy-start.20
  656.2 30.4 %all-gather.19.cloned.1.call-start = ((), (), s32[]{:S(2)}) async-start(), calls=%async_computation.21 | async-start | bytes 6291456 | tf_op jit(solution)/shard_map/all_gather | solution.py:26
  656.7 110.0 %reduce-scatter.30.cloned.1.call-start = ((), (), s32[]{:S(2)}) async-start(), calls=%async_computation.30 | async-start | bytes 5242880 | tf_op jit(solution)/shard_map/reduce_scatter | solution.py:22
  678.8 167.9 %reduce-scatter.22.cloned.1.call-start = ((), (), s32[]{:S(2)}) async-start(), calls=%async_computation.22 | async-start | bytes 5242880 | tf_op jit(solution)/shard_map/reduce_scatter | solution.py:22
  696.7 240.2 %reduce-scatter.44.cloned.1.call-start = ((), (), s32[]{:S(2)}) async-start(), calls=%async_computation.37 | async-start | bytes 10485760 | tf_op jit(solution)/shard_map/reduce_scatter | solution.py:271
  707.5 268.1 %reduce-scatter.38.cloned.1.call-start = ((), (), s32[]{:S(2)}) async-start(), calls=%async_computation.34 | async-start | bytes 2621440 | tf_op jit(solution)/shard_map/reduce_scatter | solution.py:268
  712.8 352.7 %reduce-scatter.40.cloned.1.call-start = ((), (), s32[]{:S(2)}) async-start(), calls=%async_computation.35 | async-start | bytes 10485760 | tf_op jit(solution)/shard_map/reduce_scatter | solution.py:269
  723.5 431.8 %reduce-scatter.42.cloned.1.call-start = ((), (), s32[]{:S(2)}) async-start(), calls=%async_computation.36 | async-start | bytes 10485760 | tf_op jit(solution)/shard_map/reduce_scatter | solution.py:270
  734.3 459.8 %reduce-scatter.32.cloned.1.call-start = ((), (), s32[]{:S(2)}) async-start(), calls=%async_computation.31 | async-start | bytes 2621440 | tf_op jit(solution)/shard_map/reduce_scatter | solution.py:265
  738.9 494.0 %reduce-scatter.34.cloned.1.call-start = ((), (), s32[]{:S(2)}) async-start(), calls=%async_computation.32 | async-start | bytes 2621440 | tf_op jit(solution)/shard_map/reduce_scatter | solution.py:266
  743.7 4.6 copy-start.35
  743.7 23.0 %copy-start.4 = (bf16[1024,256]{1,0:T(8,128)(2,1)S(1)}, bf16[1024,256]{1,0:T(8,128)(2,1)}, u32[]{:S(2)}) copy-start(bf16[1024,256]{1,0:T(8,128)(2,1)} %param.13) | copy-start | bytes 1572868
  743.7 23.0 %copy-start.23 = (f32[1024]{0:T(1024)S(1)}, f32[1024]{0:T(1024)}, u32[]{:S(2)}) copy-start(f32[1024]{0:T(1024)} %copy-done.22) | copy-start | bytes 12292
  743.7 23.0 %copy-start.26 = (f32[256]{0:T(256)S(1)}, f32[256]{0:T(256)}, u32[]{:S(2)}) copy-start(f32[256]{0:T(256)} %param.14) | copy-start | bytes 3076
  743.7 527.9 %reduce-scatter.36.cloned.1.call-start = ((), (), s32[]{:S(2)}) async-start(), calls=%async_computation.33 | async-start | bytes 2621440 | tf_op jit(solution)/shard_map/reduce_scatter | solution.py:267
  748.9 522.7 %copy-start.1 = (bf16[512,1024]{1,0:T(8,128)(2,1)S(1)}, bf16[512,1024]{1,0:T(8,128)(2,1)}, u32[]{:S(2)}) copy-start(bf16[512,1024]{1,0:T(8,128)(2,1)} %param.19) | copy-start | bytes 3145732
  (11 other events, 26.6 us)
Sparse Core Ops, SparseCore 0:
  36.1 47.6 all-gather.12
  93.0 11.9 reduce-scatter.15
  138.5 10.3 all-gather.14
  153.5 77.9 reduce-scatter.17
  232.9 47.0 all-gather.20
  282.0 44.8 all-gather.16
  329.2 14.4 reduce-scatter.23
  346.0 26.2 reduce-scatter.19
  381.7 21.1 all-gather.22
  417.1 77.9 reduce-scatter.25
  523.5 46.4 all-gather.24
  574.2 7.7 reduce-scatter.27
  656.3 13.3 all-gather.26
  671.7 14.8 all-gather.18
  688.7 77.9 reduce-scatter.29
  768.9 77.7 reduce-scatter.21
  850.2 86.6 reduce-scatter.43
  940.3 35.1 reduce-scatter.37
  979.2 86.3 reduce-scatter.39
  1069.0 86.3 reduce-scatter.41
  1158.9 35.1 reduce-scatter.31
  1197.7 35.1 reduce-scatter.33
  1236.4 35.1 reduce-scatter.35
